TPU v7x, 32 devices: a whole 2x2x4 slice. The times are simulated.
32 devices in a mesh: dp: 4 (over y, x), frame: 2 (over core), tensor: 4 (over z).
Axes of the slice: x: 2, y: 2, z: 4, core: 2. Of those that a mesh axis runs over, the one named last changes fastest.
Arguments:
- tokens: bfloat16 [8, 8, 256, 1024], P('dp', ('frame', 'tensor')), may hold values from -6 to 6
- out_grad: bfloat16 [8, 8, 256, 1024], P('dp', ('frame', 'tensor')), may hold values from -6 to 6
- noise_index: int32 [8, 8], P('dp', 'frame'), may hold values from 0 to 999, as said below
- qkv_weight: bfloat16 [1024, 3, 1024], P(('dp', 'frame'), None, 'tensor'), may hold values from -0.1875 to 0.1875
- out_weight: bfloat16 [1024, 1024], P(('dp', 'frame'), 'tensor'), may hold values from -0.75 to 0.75
- up_weight: bfloat16 [1024, 4096], P(('dp', 'frame'), 'tensor'), may hold values from -0.1875 to 0.1875
- down_weight: bfloat16 [1024, 4096], P(('dp', 'frame'), 'tensor'), may hold values from -0.09375 to 0.09375
- ada_weight: bfloat16 [1024, 6, 1024], P(('dp', 'frame'), None, 'tensor'), may hold values from -0.25 to 0.25
Outputs:
- result: bfloat16 [8, 8, 256, 1024], P('dp', ('frame', 'tensor'))
- input_grad: bfloat16 [8, 8, 256, 1024], P('dp', ('frame', 'tensor'))
- qkv_grad: float32 [1024, 3, 1024], P(('dp', 'frame'), None, 'tensor')
- out_weight_grad: float32 [1024, 1024], P(('dp', 'frame'), 'tensor')
- up_grad: float32 [1024, 4096], P(('dp', 'frame'), 'tensor')
- down_grad: float32 [1024, 4096], P(('dp', 'frame'), 'tensor')
- ada_grad: float32 [1024, 6, 1024], P(('dp', 'frame'), None, 'tensor')
Inputs may be any that keep to these rules, and one draw needn't show every extreme that they name: `noise_index`: each frame's noise level, most often near 1000 - 1.
All inputs are finite; a program needn't handle non-finite values.
Results may differ from a plain program's by a relative error of at most 0.018.
Values may be sent and summed in bfloat16 or wider, within the bound.
A program may use at most 192 MiB of HBM per device.

v0:
```python
import math
import jax
import jax.numpy as jnp
from jax import lax
from jax.sharding import PartitionSpec as P

HEAD_DIM = 64
epsilon = 1e-06
highest = lax.Precision.HIGHEST


def normalize(values):
    center = values - jnp.mean(values, axis=-1, keepdims=True)
    spread = jnp.mean(center * center, axis=-1, keepdims=True)
    inverse = lax.rsqrt(spread + epsilon)
    return (center * inverse, inverse)


def norm_back(upstream, normed, inverse):
    upstream_mean = jnp.mean(upstream, axis=-1, keepdims=True)
    product_mean = jnp.mean(upstream * normed, axis=-1, keepdims=True)
    return inverse * (upstream - upstream_mean - normed * product_mean)


def level_embedding(levels, model_width):
    halfway = model_width // 2
    frequency = jnp.exp(-math.log(10000.0) * jnp.arange(halfway, dtype=jnp.float32) / halfway)
    angles = levels.astype(jnp.float32)[..., None] * frequency
    return jnp.concatenate([jnp.cos(angles), jnp.sin(angles)], axis=-1)


def gelu_tanh(values):
    return jax.nn.gelu(values, approximate=True)


def on_device(
    tokens, out_grad, noise_index, qkv_weight, out_weight, up_weight, down_weight, ada_weight
):
    model_width = tokens.shape[-1]
    patches_here = tokens.shape[2]
    local_width = qkv_weight.shape[2]
    hidden_local = up_weight.shape[1]
    heads_here = local_width // HEAD_DIM
    scaling = HEAD_DIM ** (-0.5)
    shards = (qkv_weight, out_weight, up_weight, down_weight, ada_weight)

    def fetch_weights():
        fetched = (
            lax.all_gather(shards[0], ("dp", "frame"), axis=0, tiled=True),
            lax.all_gather(shards[1], ("dp", "frame"), axis=0, tiled=True),
            lax.all_gather(shards[2], ("dp", "frame"), axis=0, tiled=True),
            lax.all_gather(shards[3], ("dp", "frame"), axis=0, tiled=True),
            lax.all_gather(shards[4], ("dp", "frame"), axis=0, tiled=True),
        )
        return fetched

    def one_clip(totals, inputs, weights):
        clip_tokens, clip_cotangent, clip_levels = inputs
        joint_weight, mixer_weight, upward_weight, downward_weight, adaptive_weight = weights
        condition = jax.nn.silu(level_embedding(clip_levels, model_width)).astype(jnp.bfloat16)
        columns = jnp.einsum(
            "fd,dkc->fkc", condition, adaptive_weight, preferred_element_type=jnp.float32
        )
        modulation = lax.all_to_all(columns, "tensor", split_axis=0, concat_axis=2, tiled=True)[
            :, :, None, :
        ]
        residual = clip_tokens.astype(jnp.float32)
        normed_one, inverse_one = normalize(residual)
        entering_one = (normed_one * (1.0 + modulation[:, 1]) + modulation[:, 0]).astype(
            jnp.bfloat16
        )
        gathered_one = lax.all_gather(entering_one, "tensor", axis=0, tiled=True)
        token_count = gathered_one.shape[0] * patches_here
        flat_one = gathered_one.reshape(token_count, model_width)
        projected = jnp.einsum(
            "rd,dkc->rkc", flat_one, joint_weight, preferred_element_type=jnp.float32
        ).astype(jnp.bfloat16)
        keys_all, values_all = (
            lax.all_gather(projected[:, 1], "frame", axis=0, tiled=True),
            lax.all_gather(projected[:, 2], "frame", axis=0, tiled=True),
        )
        key_heads = keys_all.reshape(-1, heads_here, HEAD_DIM)
        value_heads = values_all.reshape(-1, heads_here, HEAD_DIM)
        block_rows = min(512, token_count)
        block_count = token_count // block_rows
        query_blocks = projected[:, 0].reshape(block_count, block_rows, heads_here, HEAD_DIM)

        def attend(query_block):
            scores = (
                jnp.einsum(
                    "qhe,khe->hqk", query_block, key_heads, preferred_element_type=jnp.float32
                )
                * scaling
            )
            largest = jnp.max(scores, axis=-1, keepdims=True)
            raised = jnp.exp(scores - largest)
            totals_row = jnp.sum(raised, axis=-1, keepdims=True)
            probs_low = (raised / totals_row).astype(jnp.bfloat16)
            outputs = jnp.einsum(
                "hqk,khe->qhe", probs_low, value_heads, preferred_element_type=jnp.float32
            )
            return (outputs.astype(jnp.bfloat16), (largest + jnp.log(totals_row))[..., 0])

        attended_blocks, log_totals = lax.map(attend, query_blocks)
        attended = attended_blocks.reshape(token_count, local_width)
        partial_one = jnp.einsum(
            "rc,oc->ro", attended, mixer_weight, preferred_element_type=jnp.float32
        )
        branch_one = lax.psum_scatter(
            partial_one.reshape(-1, patches_here, model_width),
            "tensor",
            scatter_dimension=0,
            tiled=True,
        )
        middle = residual + modulation[:, 2] * branch_one
        normed_two, inverse_two = normalize(middle)
        entering_two = (normed_two * (1.0 + modulation[:, 4]) + modulation[:, 3]).astype(
            jnp.bfloat16
        )
        upstream = clip_cotangent.astype(jnp.float32)
        flat_two = lax.all_gather(entering_two, "tensor", axis=0, tiled=True).reshape(
            token_count, model_width
        )
        up_values = jnp.dot(flat_two, upward_weight, preferred_element_type=jnp.float32)
        hidden = gelu_tanh(up_values).astype(jnp.bfloat16)
        partial_two = jnp.einsum(
            "rf,of->ro", hidden, downward_weight, preferred_element_type=jnp.float32
        )
        branch_two = lax.psum_scatter(
            partial_two.reshape(-1, patches_here, model_width).astype(jnp.bfloat16),
            "tensor",
            scatter_dimension=0,
            tiled=True,
        ).astype(jnp.float32)
        grad_branch_two = (modulation[:, 5] * upstream).astype(jnp.bfloat16)
        grad_two_all = lax.all_gather(grad_branch_two, "tensor", axis=0, tiled=True).reshape(
            token_count, model_width
        )
        output = (middle + modulation[:, 5] * branch_two).astype(jnp.bfloat16)
        grad_gate_two = jnp.sum(upstream * branch_two, axis=1)
        grad_hidden = jnp.dot(grad_two_all, downward_weight, preferred_element_type=jnp.float32)
        down_total = jnp.einsum(
            "ro,rf->of", grad_two_all, hidden, preferred_element_type=jnp.float32
        )
        _, gelu_pullback = jax.vjp(gelu_tanh, up_values)
        grad_up = gelu_pullback(grad_hidden)[0].astype(jnp.bfloat16)
        up_total = jnp.einsum("rd,rf->df", flat_two, grad_up, preferred_element_type=jnp.float32)
        partial_back_two = jnp.einsum(
            "rf,df->rd", grad_up, upward_weight, preferred_element_type=jnp.float32
        ).reshape(-1, patches_here, model_width)
        grad_entering_two = lax.psum_scatter(
            partial_back_two.astype(jnp.bfloat16), "tensor", scatter_dimension=0, tiled=True
        ).astype(jnp.float32)
        grad_shift_two = jnp.sum(grad_entering_two, axis=1)
        grad_scale_two = jnp.sum(grad_entering_two * normed_two, axis=1)
        grad_middle = upstream + norm_back(
            grad_entering_two * (1.0 + modulation[:, 4]), normed_two, inverse_two
        )
        grad_gate_one = jnp.sum(grad_middle * branch_one, axis=1)
        grad_branch_one = (modulation[:, 2] * grad_middle).astype(jnp.bfloat16)
        grad_one_all = lax.all_gather(grad_branch_one, "tensor", axis=0, tiled=True).reshape(
            token_count, model_width
        )
        grad_attended = jnp.dot(
            grad_one_all, mixer_weight, preferred_element_type=jnp.float32
        ).astype(jnp.bfloat16)
        mixer_total = jnp.einsum(
            "ro,rc->oc", grad_one_all, attended, preferred_element_type=jnp.float32
        )
        grad_blocks = grad_attended.reshape(block_count, block_rows, heads_here, HEAD_DIM)

        def attend_back(carried, pieces):
            key_sum, value_sum = carried
            query_block, grad_block, log_block = pieces
            scores = (
                jnp.einsum(
                    "qhe,khe->hqk", query_block, key_heads, preferred_element_type=jnp.float32
                )
                * scaling
            )
            probs = jnp.exp(scores - log_block[..., None])
            grad_probs = jnp.einsum(
                "qhe,khe->hqk", grad_block, value_heads, preferred_element_type=jnp.float32
            )
            value_sum = value_sum + jnp.einsum(
                "hqk,qhe->khe",
                probs.astype(jnp.bfloat16),
                grad_block,
                preferred_element_type=jnp.float32,
            )
            row_terms = jnp.sum(probs * grad_probs, axis=-1, keepdims=True)
            grad_scores = (probs * (grad_probs - row_terms)).astype(jnp.bfloat16)
            grad_queries = (
                jnp.einsum(
                    "hqk,khe->qhe", grad_scores, key_heads, preferred_element_type=jnp.float32
                )
                * scaling
            )
            key_sum = (
                key_sum
                + jnp.einsum(
                    "hqk,qhe->khe", grad_scores, query_block, preferred_element_type=jnp.float32
                )
                * scaling
            )
            return ((key_sum, value_sum), grad_queries)

        zeros_keys = jnp.zeros(key_heads.shape, jnp.float32)
        (key_grads, value_grads), query_grads = lax.scan(
            attend_back, (zeros_keys, zeros_keys), (query_blocks, grad_blocks, log_totals)
        )
        key_own, value_own = (
            lax.psum_scatter(
                key_grads.reshape(-1, local_width).astype(jnp.bfloat16),
                "frame",
                scatter_dimension=0,
                tiled=True,
            ).astype(jnp.float32),
            lax.psum_scatter(
                value_grads.reshape(-1, local_width).astype(jnp.bfloat16),
                "frame",
                scatter_dimension=0,
                tiled=True,
            ).astype(jnp.float32),
        )
        grad_projected = jnp.stack(
            [query_grads.reshape(token_count, local_width), key_own, value_own], axis=1
        ).astype(jnp.bfloat16)
        joint_total = jnp.einsum(
            "rd,rkc->dkc", flat_one, grad_projected, preferred_element_type=jnp.float32
        )
        partial_back_one = jnp.einsum(
            "rkc,dkc->rd", grad_projected, joint_weight, preferred_element_type=jnp.float32
        )
        grad_entering_one = lax.psum_scatter(
            partial_back_one.reshape(-1, patches_here, model_width).astype(jnp.bfloat16),
            "tensor",
            scatter_dimension=0,
            tiled=True,
        ).astype(jnp.float32)
        grad_shift_one = jnp.sum(grad_entering_one, axis=1)
        grad_scale_one = jnp.sum(grad_entering_one * normed_one, axis=1)
        grad_input = grad_middle + norm_back(
            grad_entering_one * (1.0 + modulation[:, 1]), normed_one, inverse_one
        )
        grad_modulation = jnp.stack(
            [
                grad_shift_one,
                grad_scale_one,
                grad_gate_one,
                grad_shift_two,
                grad_scale_two,
                grad_gate_two,
            ],
            axis=1,
        )
        grad_columns = lax.all_to_all(
            grad_modulation, "tensor", split_axis=2, concat_axis=0, tiled=True
        )
        adaptive_total = jnp.einsum(
            "fd,fkc->dkc", condition.astype(jnp.float32), grad_columns, precision=highest
        )
        updates = (joint_total, mixer_total, up_total, down_total, adaptive_total)
        totals = tuple((total + update for total, update in zip(totals, updates)))
        return (totals, (output, grad_input.astype(jnp.bfloat16)))

    initial = (
        jnp.zeros((model_width, 3, local_width), jnp.float32),
        jnp.zeros((model_width, local_width), jnp.float32),
        jnp.zeros((model_width, hidden_local), jnp.float32),
        jnp.zeros((model_width, hidden_local), jnp.float32),
        jnp.zeros((model_width, 6, local_width), jnp.float32),
    )

    def micro_step(totals, inputs):
        return one_clip(totals, inputs, fetch_weights())

    totals, (result, input_grad) = lax.scan(micro_step, initial, (tokens, out_grad, noise_index))
    summed = (
        lax.psum_scatter(
            totals[0].astype(jnp.bfloat16), ("dp", "frame"), scatter_dimension=0, tiled=True
        ).astype(jnp.float32),
        lax.psum_scatter(
            totals[1].astype(jnp.bfloat16), ("dp", "frame"), scatter_dimension=0, tiled=True
        ).astype(jnp.float32),
        lax.psum_scatter(
            totals[2].astype(jnp.bfloat16), ("dp", "frame"), scatter_dimension=0, tiled=True
        ).astype(jnp.float32),
        lax.psum_scatter(
            totals[3].astype(jnp.bfloat16), ("dp", "frame"), scatter_dimension=0, tiled=True
        ).astype(jnp.float32),
        lax.psum_scatter(
            totals[4].astype(jnp.bfloat16), ("dp", "frame"), scatter_dimension=0, tiled=True
        ).astype(jnp.float32),
    )
    return (result, input_grad, summed[0], summed[1], summed[2], summed[3], summed[4])


def solution(mesh):
    return jax.shard_map(
        on_device,
        mesh=mesh,
        in_specs=(
            P("dp", ("frame", "tensor"), None, None),
            P("dp", ("frame", "tensor"), None, None),
            P("dp", "frame"),
            P(("dp", "frame"), None, "tensor"),
            P(("dp", "frame"), "tensor"),
            P(("dp", "frame"), "tensor"),
            P(("dp", "frame"), "tensor"),
            P(("dp", "frame"), None, "tensor"),
        ),
        out_specs=(
            P("dp", ("frame", "tensor"), None, None),
            P("dp", ("frame", "tensor"), None, None),
            P(("dp", "frame"), None, "tensor"),
            P(("dp", "frame"), "tensor"),
            P(("dp", "frame"), "tensor"),
            P(("dp", "frame"), "tensor"),
            P(("dp", "frame"), None, "tensor"),
        ),
        check_vma=False,
    )
```

profile of v0, /device:TPU:0, one launch (start us, length us, event | category | flops | bytes accessed | tf_op | source)
XLA Modules:
  0.0 1683.6 jit_solution(13666818316146468677)
XLA Ops:
  8.1 1450.1 %while.83 = (s32[]{:T(128)}, f32[1024,3,256]{2,0,1:T(8,128)}, f32[1024,256]{1,0:T(8,128)}, f32[1024,1024]{1,0:T(8,128)}, f32[1024,1024]{1,0:T(8,128)}, /*index=5...) while((s32[]{:T(128)}, f32[1024,3,256]{2,0,1:T(8,128)}, ...), condition=%wide.region_28.29_spmd.clone, body=%wide.region_0.28_spmd.clone.sunk | while | flops 23346327552 | bytes 683999296 | solution.py:278
  13.2 32.8 %all-gather.19.cloned.1.call-done = bf16[1024,6,256]{2,0,1:T(8,128)(2,1)} async-done(((bf16[128,6,256]{2,0,1:T(8,128)(2,1)}), bf16[1024,6,256]{2,0,1:T(8,128)(2,1)}) %all-gather.19.cloned.1.call-update) | async-done | bytes 3145744 | tf_op jit(solution)/shard_map/while/body/eval_jaxpr/all_gather | solution.py:53
  61.7 11.8 all-gather.23.cloned.1.call-done
  73.5 47.8 %all-gather.21.cloned.1.call-done = bf16[4,256,1024]{2,1,0:T(8,128)(2,1)} async-done(((bf16[1,256,1024]{2,1,0:T(8,128)(2,1)}), bf16[4,256,1024]{2,1,0:T(8,128)(2,1)}) %all-gather.21.cloned.1.call-update) | async-done | bytes 2097168 | tf_op jit(solution)/shard_map/while/body/eval_jaxpr/all_gather | solution.py:72
  127.0 10.8 all_gather.87
  148.1 20.5 %while.84 = (s32[]{:T(128)}, bf16[2,512,4,64]{1,3,2,0:T(8,128)(2,1)S(1)}, f32[2,4,512]{2,1,0:T(4,128)S(1)}, bf16[2,512,4,64]{1,3,2,0:T(8,128)(2,1)S(1)}, bf16[20...) while((s32[]{:T(128)}, bf16[2,512,4,64]{1,3,2,0:T(8,128)(2,1)S(1)}, ...), condition=%wide.region_6.6_spmd, body=%wide.region_3.5_spmd.sunk | while | flops 1111619584 | bytes 53018720 | solution.py:104
  180.4 74.6 %reduce-scatter.22.cloned.1.call-done = f32[1,256,1024]{2,1,0:T(8,128)} async-done(((f32[4,256,1024]{2,1,0:T(8,128)}), f32[1,256,1024]{2,1,0:T(8,128)}) %reduce-scatter.22.cloned.1.call-update) | async-done | bytes 1048592 | tf_op jit(solution)/shard_map/while/body/eval_jaxpr/reduce_scatter | solution.py:109
  259.2 25.9 %all-gather.31.cloned.1.call-done = bf16[1024,1024]{1,0:T(8,128)(2,1)} async-done(((bf16[128,1024]{1,0:T(8,128)(2,1)}), bf16[1024,1024]{1,0:T(8,128)(2,1)}) %all-gather.31.cloned.1.call-update) | async-done | bytes 2097168 | tf_op jit(solution)/shard_map/while/body/eval_jaxpr/all_gather | solution.py:52
  285.1 47.8 %all-gather.29.cloned.1.call-done = bf16[4,256,1024]{2,1,0:T(8,128)(2,1)} async-done(((bf16[1,256,1024]{2,1,0:T(8,128)(2,1)}), bf16[4,256,1024]{2,1,0:T(8,128)(2,1)}) %all-gather.29.cloned.1.call-update) | async-done | bytes 2097168 | tf_op jit(solution)/shard_map/while/body/eval_jaxpr/all_gather | solution.py:136
  339.5 22.0 %all-gather.35.cloned.1.call-done = bf16[1024,1024]{1,0:T(8,128)(2,1)} async-done(((bf16[128,1024]{1,0:T(8,128)(2,1)}), bf16[1024,1024]{1,0:T(8,128)(2,1)}) %all-gather.35.cloned.1.call-update) | async-done | bytes 2097168 | tf_op jit(solution)/shard_map/while/body/eval_jaxpr/all_gather | solution.py:51
  361.5 47.7 %all-gather.33.cloned.1.call-done = bf16[4,256,1024]{2,1,0:T(8,128)(2,1)} async-done(((bf16[1,256,1024]{2,1,0:T(8,128)(2,1)}), bf16[4,256,1024]{2,1,0:T(8,128)(2,1)}) %all-gather.33.cloned.1.call-update) | async-done | bytes 2097168 | tf_op jit(solution)/shard_map/while/body/eval_jaxpr/all_gather | solution.py:121
  409.1 10.0 fusion.215
  429.9 35.6 %reduce-scatter.24.cloned.1.call-done = bf16[1,256,1024]{2,1,0:T(8,128)(2,1)} async-done(((bf16[4,256,1024]{2,1,0:T(8,128)(2,1)}), bf16[1,256,1024]{2,1,0:T(8,128)(2,1)}) %reduce-scatter.24.cloned.1.call-update) | async-done | bytes 524304 | tf_op jit(solution)/shard_map/while/body/eval_jaxpr/reduce_scatter | solution.py:151
  468.0 42.5 %reduce-scatter.26.cloned.1.call-done = bf16[1,256,1024]{2,1,0:T(8,128)(2,1)} async-done(((bf16[4,256,1024]{2,1,0:T(8,128)(2,1)}), bf16[1,256,1024]{2,1,0:T(8,128)(2,1)}) %reduce-scatter.26.cloned.1.call-update) | async-done | bytes 524304 | tf_op jit(solution)/shard_map/while/body/eval_jaxpr/reduce_scatter | solution.py:129
  515.9 44.7 %all-gather.37.cloned.1.call-done = bf16[4,256,1024]{2,1,0:T(8,128)(2,1)} async-done(((bf16[1,256,1024]{2,1,0:T(8,128)(2,1)}), bf16[4,256,1024]{2,1,0:T(8,128)(2,1)}) %all-gather.37.cloned.1.call-update) | async-done | bytes 2097168 | tf_op jit(solution)/shard_map/while/body/eval_jaxpr/all_gather | solution.py:161
  568.1 72.0 %while.85 = (s32[]{:T(128)}, f32[2048,4,64]{0,2,1:T(8,128)}, f32[2048,4,64]{0,2,1:T(8,128)}, bf16[2,512,4,64]{1,3,2,0:T(8,128)(2,1)}, bf16[2,512,4,64]{1,3,2,0:T...) while((s32[]{:T(128)}, f32[2048,4,64]{0,2,1:T(8,128)}, ...), condition=%wide.region_15.15_spmd.clone, body=%wide.region_13.14_spmd.clone.sunk | while | flops 2737436672 | bytes 176742640 | solution.py:209
  574.9 8.0 multiply_reduce_fusion.11
  582.9 10.5 multiply_convert_fusion.12
  610.6 8.0 multiply_reduce_fusion.11
  618.6 10.5 multiply_convert_fusion.12
  650.5 11.7 reduce-scatter.28.cloned.1.call-done
  686.1 25.7 %reduce-scatter.32.cloned.1.call-done = bf16[1,256,1024]{2,1,0:T(8,128)(2,1)} async-done(((bf16[4,256,1024]{2,1,0:T(8,128)(2,1)}), bf16[1,256,1024]{2,1,0:T(8,128)(2,1)}) %reduce-scatter.32.cloned.1.call-update) | async-done | bytes 524304 | tf_op jit(solution)/shard_map/while/body/eval_jaxpr/reduce_scatter | solution.py:235
  738.3 28.3 %all-gather.19.cloned.1.call-done = bf16[1024,6,256]{2,0,1:T(8,128)(2,1)} async-done(((bf16[128,6,256]{2,0,1:T(8,128)(2,1)}), bf16[1024,6,256]{2,0,1:T(8,128)(2,1)}) %all-gather.19.cloned.1.call-update) | async-done | bytes 3145744 | tf_op jit(solution)/shard_map/while/body/eval_jaxpr/all_gather | solution.py:53
  782.4 11.7 all-gather.23.cloned.1.call-done
  794.0 47.8 %all-gather.21.cloned.1.call-done = bf16[4,256,1024]{2,1,0:T(8,128)(2,1)} async-done(((bf16[1,256,1024]{2,1,0:T(8,128)(2,1)}), bf16[4,256,1024]{2,1,0:T(8,128)(2,1)}) %all-gather.21.cloned.1.call-update) | async-done | bytes 2097168 | tf_op jit(solution)/shard_map/while/body/eval_jaxpr/all_gather | solution.py:72
  847.6 10.8 all_gather.87
  868.7 20.5 %while.84 = (s32[]{:T(128)}, bf16[2,512,4,64]{1,3,2,0:T(8,128)(2,1)S(1)}, f32[2,4,512]{2,1,0:T(4,128)S(1)}, bf16[2,512,4,64]{1,3,2,0:T(8,128)(2,1)S(1)}, bf16[20...) while((s32[]{:T(128)}, bf16[2,512,4,64]{1,3,2,0:T(8,128)(2,1)S(1)}, ...), condition=%wide.region_6.6_spmd, body=%wide.region_3.5_spmd.sunk | while | flops 1111619584 | bytes 53018720 | solution.py:104
  901.0 74.6 %reduce-scatter.22.cloned.1.call-done = f32[1,256,1024]{2,1,0:T(8,128)} async-done(((f32[4,256,1024]{2,1,0:T(8,128)}), f32[1,256,1024]{2,1,0:T(8,128)}) %reduce-scatter.22.cloned.1.call-update) | async-done | bytes 1048592 | tf_op jit(solution)/shard_map/while/body/eval_jaxpr/reduce_scatter | solution.py:109
  979.5 26.3 %all-gather.31.cloned.1.call-done = bf16[1024,1024]{1,0:T(8,128)(2,1)} async-done(((bf16[128,1024]{1,0:T(8,128)(2,1)}), bf16[1024,1024]{1,0:T(8,128)(2,1)}) %all-gather.31.cloned.1.call-update) | async-done | bytes 2097168 | tf_op jit(solution)/shard_map/while/body/eval_jaxpr/all_gather | solution.py:52
  1005.7 47.7 %all-gather.29.cloned.1.call-done = bf16[4,256,1024]{2,1,0:T(8,128)(2,1)} async-done(((bf16[1,256,1024]{2,1,0:T(8,128)(2,1)}), bf16[4,256,1024]{2,1,0:T(8,128)(2,1)}) %all-gather.29.cloned.1.call-update) | async-done | bytes 2097168 | tf_op jit(solution)/shard_map/while/body/eval_jaxpr/all_gather | solution.py:136
  1060.0 22.0 %all-gather.35.cloned.1.call-done = bf16[1024,1024]{1,0:T(8,128)(2,1)} async-done(((bf16[128,1024]{1,0:T(8,128)(2,1)}), bf16[1024,1024]{1,0:T(8,128)(2,1)}) %all-gather.35.cloned.1.call-update) | async-done | bytes 2097168 | tf_op jit(solution)/shard_map/while/body/eval_jaxpr/all_gather | solution.py:51
  1081.9 47.7 %all-gather.33.cloned.1.call-done = bf16[4,256,1024]{2,1,0:T(8,128)(2,1)} async-done(((bf16[1,256,1024]{2,1,0:T(8,128)(2,1)}), bf16[4,256,1024]{2,1,0:T(8,128)(2,1)}) %all-gather.33.cloned.1.call-update) | async-done | bytes 2097168 | tf_op jit(solution)/shard_map/while/body/eval_jaxpr/all_gather | solution.py:121
  1129.6 10.0 fusion.215
  1150.4 35.5 %reduce-scatter.24.cloned.1.call-done = bf16[1,256,1024]{2,1,0:T(8,128)(2,1)} async-done(((bf16[4,256,1024]{2,1,0:T(8,128)(2,1)}), bf16[1,256,1024]{2,1,0:T(8,128)(2,1)}) %reduce-scatter.24.cloned.1.call-update) | async-done | bytes 524304 | tf_op jit(solution)/shard_map/while/body/eval_jaxpr/reduce_scatter | solution.py:151
  1188.5 42.6 %reduce-scatter.26.cloned.1.call-done = bf16[1,256,1024]{2,1,0:T(8,128)(2,1)} async-done(((bf16[4,256,1024]{2,1,0:T(8,128)(2,1)}), bf16[1,256,1024]{2,1,0:T(8,128)(2,1)}) %reduce-scatter.26.cloned.1.call-update) | async-done | bytes 524304 | tf_op jit(solution)/shard_map/while/body/eval_jaxpr/reduce_scatter | solution.py:129
  1236.7 44.5 %all-gather.37.cloned.1.call-done = bf16[4,256,1024]{2,1,0:T(8,128)(2,1)} async-done(((bf16[1,256,1024]{2,1,0:T(8,128)(2,1)}), bf16[4,256,1024]{2,1,0:T(8,128)(2,1)}) %all-gather.37.cloned.1.call-update) | async-done | bytes 2097168 | tf_op jit(solution)/shard_map/while/body/eval_jaxpr/all_gather | solution.py:161
  1288.7 72.0 %while.85 = (s32[]{:T(128)}, f32[2048,4,64]{0,2,1:T(8,128)}, f32[2048,4,64]{0,2,1:T(8,128)}, bf16[2,512,4,64]{1,3,2,0:T(8,128)(2,1)}, bf16[2,512,4,64]{1,3,2,0:T...) while((s32[]{:T(128)}, f32[2048,4,64]{0,2,1:T(8,128)}, ...), condition=%wide.region_15.15_spmd.clone, body=%wide.region_13.14_spmd.clone.sunk | while | flops 2737436672 | bytes 176742640 | solution.py:209
  1295.5 8.0 multiply_reduce_fusion.11
  1303.5 10.5 multiply_convert_fusion.12
  1331.2 8.0 multiply_reduce_fusion.11
  1339.2 10.5 multiply_convert_fusion.12
  1371.1 11.9 reduce-scatter.28.cloned.1.call-done
  1410.1 22.5 %reduce-scatter.32.cloned.1.call-done = bf16[1,256,1024]{2,1,0:T(8,128)(2,1)} async-done(((bf16[4,256,1024]{2,1,0:T(8,128)(2,1)}), bf16[1,256,1024]{2,1,0:T(8,128)(2,1)}) %reduce-scatter.32.cloned.1.call-update) | async-done | bytes 524304 | tf_op jit(solution)/shard_map/while/body/eval_jaxpr/reduce_scatter | solution.py:235
  1476.4 18.3 %reduce-scatter.14.cloned.1.call-done = bf16[128,256]{1,0:T(8,128)(2,1)} async-done(((bf16[1024,256]{1,0:T(8,128)(2,1)}), bf16[128,256]{1,0:T(8,128)(2,1)}) %reduce-scatter.14.cloned.1.call-update) | async-done | bytes 65552 | tf_op jit(solution)/shard_map/reduce_scatter | solution.py:283
  1496.2 39.9 %reduce-scatter.12.cloned.1.call-done = bf16[128,3,256]{2,0,1:T(8,128)(2,1)} async-done(((bf16[1024,3,256]{2,0,1:T(8,128)(2,1)}), bf16[128,3,256]{2,0,1:T(8,128)(2,1)}) %reduce-scatter.12.cloned.1.call-update) | async-done | bytes 196624 | tf_op jit(solution)/shard_map/reduce_scatter | solution.py:280
  1537.9 42.4 %reduce-scatter.16.cloned.1.call-done = bf16[128,1024]{1,0:T(8,128)(2,1)} async-done(((bf16[1024,1024]{1,0:T(8,128)(2,1)}), bf16[128,1024]{1,0:T(8,128)(2,1)}) %reduce-scatter.16.cloned.1.call-update) | async-done | bytes 262160 | tf_op jit(solution)/shard_map/reduce_scatter | solution.py:286
  1582.1 42.5 %reduce-scatter.18.cloned.1.call-done = bf16[128,1024]{1,0:T(8,128)(2,1)} async-done(((bf16[1024,1024]{1,0:T(8,128)(2,1)}), bf16[128,1024]{1,0:T(8,128)(2,1)}) %reduce-scatter.18.cloned.1.call-update) | async-done | bytes 262160 | tf_op jit(solution)/shard_map/reduce_scatter | solution.py:289
  1626.4 47.5 %reduce-scatter.20.cloned.1.call-done = bf16[128,6,256]{2,0,1:T(8,128)(2,1)} async-done(((bf16[1024,6,256]{2,0,1:T(8,128)(2,1)}), bf16[128,6,256]{2,0,1:T(8,128)(2,1)}) %reduce-scatter.20.cloned.1.call-update) | async-done | bytes 393232 | tf_op jit(solution)/shard_map/reduce_scatter | solution.py:292
  (503 shorter events, 422.8 us)
Async XLA Ops:
  8.3 37.7 %all-gather.19.cloned.1.call-start = ((), (), s32[]{:S(2)}) async-start(), calls=%async_computation.18 | async-start | bytes 3538944 | tf_op jit(solution)/shard_map/while/body/eval_jaxpr/all_gather | solution.py:53
  9.1 64.4 %all-gather.23.cloned.1.call-start = ((), (), s32[]{:S(2)}) async-start(), calls=%async_computation.20 | async-start | bytes 1769472 | tf_op jit(solution)/shard_map/while/body/eval_jaxpr/all_gather | solution.py:49
  11.7 113.4 %copy-start.32 = (f32[256]{0:T(256)}, f32[256]{0:T(256)S(1)}, u32[]{:S(2)}) copy-start(f32[256]{0:T(256)S(1)} %broadcast_multiply_fusion.11) | copy-start | bytes 3076 | tf_op jit(solution)/shard_map/while
  49.0 10.3 all-to-all-start
  53.6 67.7 %all-gather.21.cloned.1.call-start = ((), (), s32[]{:S(2)}) async-start(), calls=%async_computation.19 | async-start | bytes 2621440 | tf_op jit(solution)/shard_map/while/body/eval_jaxpr/all_gather | solution.py:72
  61.7 77.2 %all-gather.25.cloned.1.call-start = ((), (), s32[]{:S(2)}) async-start(), calls=%async_computation.21 | async-start | bytes 1572864 | tf_op jit(solution)/shard_map/while/body/eval_jaxpr/all_gather | solution.py:79
  126.3 20.3 %all-gather.27.cloned.1.call-start = ((), (), s32[]{:S(2)}) async-start(), calls=%async_computation.22 | async-start | bytes 1572864 | tf_op jit(solution)/shard_map/while/body/eval_jaxpr/all_gather | solution.py:80
  126.9 128.0 %reduce-scatter.22.cloned.1.call-start = ((), (), s32[]{:S(2)}) async-start(), calls=%async_computation.23 | async-start | bytes 5242880 | tf_op jit(solution)/shard_map/while/body/eval_jaxpr/reduce_scatter | solution.py:109
  176.8 80.8 %copy-start.38 = (f32[1,1,1,1024]{3,0,1,2:T(1,128)S(1)}, f32[1,1,1,1024]{3,0,1,2:T(1,128)}, u32[]{:S(2)}) copy-start(f32[1,1,1,1024]{3,0,1,2:T(1,128)} %get-tuple-element.818) | copy-start | bytes 12292 | tf_op jit(solution)/shard_map/while
  176.8 108.3 %all-gather.31.cloned.1.call-start = ((), (), s32[]{:S(2)}) async-start(), calls=%async_computation.25 | async-start | bytes 2359296 | tf_op jit(solution)/shard_map/while/body/eval_jaxpr/all_gather | solution.py:52
  177.5 155.4 %all-gather.29.cloned.1.call-start = ((), (), s32[]{:S(2)}) async-start(), calls=%async_computation.24 | async-start | bytes 2621440 | tf_op jit(solution)/shard_map/while/body/eval_jaxpr/all_gather | solution.py:136
  179.6 181.9 %all-gather.35.cloned.1.call-start = ((), (), s32[]{:S(2)}) async-start(), calls=%async_computation.27 | async-start | bytes 2359296 | tf_op jit(solution)/shard_map/while/body/eval_jaxpr/all_gather | solution.py:51
  180.3 228.8 %all-gather.33.cloned.1.call-start = ((), (), s32[]{:S(2)}) async-start(), calls=%async_computation.26 | async-start | bytes 2621440 | tf_op jit(solution)/shard_map/while/body/eval_jaxpr/all_gather | solution.py:121
  258.6 206.9 %reduce-scatter.24.cloned.1.call-start = ((), (), s32[]{:S(2)}) async-start(), calls=%async_computation.28 | async-start | bytes 2621440 | tf_op jit(solution)/shard_map/while/body/eval_jaxpr/reduce_scatter | solution.py:151
  422.9 87.6 %reduce-scatter.26.cloned.1.call-start = ((), (), s32[]{:S(2)}) async-start(), calls=%async_computation.29 | async-start | bytes 2621440 | tf_op jit(solution)/shard_map/while/body/eval_jaxpr/reduce_scatter | solution.py:129
  429.9 130.7 %copy-start.11 = (bf16[1024,256]{1,0:T(8,128)(2,1)S(1)}, bf16[1024,256]{1,0:T(8,128)(2,1)}, u32[]{:S(2)}) copy-start(bf16[1024,256]{1,0:T(8,128)(2,1)} %all_gather.87) | copy-start | bytes 1572868 | tf_op jit(solution)/shard_map/while
  429.9 130.7 %all-gather.37.cloned.1.call-start = ((), (), s32[]{:S(2)}) async-start(), calls=%async_computation.30 | async-start | bytes 2621440 | tf_op jit(solution)/shard_map/while/body/eval_jaxpr/all_gather | solution.py:161
  515.6 134.9 %reduce-scatter.30.cloned.1.call-start = ((), (), s32[]{:S(2)}) async-start(), calls=%async_computation.32 | async-start | bytes 1572864 | tf_op jit(solution)/shard_map/while/body/eval_jaxpr/reduce_scatter | solution.py:213
  643.2 19.1 %reduce-scatter.28.cloned.1.call-start = ((), (), s32[]{:S(2)}) async-start(), calls=%async_computation.31 | async-start | bytes 1572864 | tf_op jit(solution)/shard_map/while/body/eval_jaxpr/reduce_scatter | solution.py:219
  646.5 65.3 %reduce-scatter.32.cloned.1.call-start = ((), (), s32[]{:S(2)}) async-start(), calls=%async_computation.33 | async-start | bytes 2621440 | tf_op jit(solution)/shard_map/while/body/eval_jaxpr/reduce_scatter | solution.py:235
  717.7 8.9 all-to-all-start.1
  733.7 32.9 %all-gather.19.cloned.1.call-start = ((), (), s32[]{:S(2)}) async-start(), calls=%async_computation.18 | async-start | bytes 3538944 | tf_op jit(solution)/shard_map/while/body/eval_jaxpr/all_gather | solution.py:53
  734.3 59.7 %all-gather.23.cloned.1.call-start = ((), (), s32[]{:S(2)}) async-start(), calls=%async_computation.20 | async-start | bytes 1769472 | tf_op jit(solution)/shard_map/while/body/eval_jaxpr/all_gather | solution.py:49
  736.8 108.9 %copy-start.32 = (f32[256]{0:T(256)}, f32[256]{0:T(256)S(1)}, u32[]{:S(2)}) copy-start(f32[256]{0:T(256)S(1)} %broadcast_multiply_fusion.11) | copy-start | bytes 3076 | tf_op jit(solution)/shard_map/while
  769.7 10.3 all-to-all-start
  774.3 67.6 %all-gather.21.cloned.1.call-start = ((), (), s32[]{:S(2)}) async-start(), calls=%async_computation.19 | async-start | bytes 2621440 | tf_op jit(solution)/shard_map/while/body/eval_jaxpr/all_gather | solution.py:72
  782.3 77.2 %all-gather.25.cloned.1.call-start = ((), (), s32[]{:S(2)}) async-start(), calls=%async_computation.21 | async-start | bytes 1572864 | tf_op jit(solution)/shard_map/while/body/eval_jaxpr/all_gather | solution.py:79
  846.8 20.4 %all-gather.27.cloned.1.call-start = ((), (), s32[]{:S(2)}) async-start(), calls=%async_computation.22 | async-start | bytes 1572864 | tf_op jit(solution)/shard_map/while/body/eval_jaxpr/all_gather | solution.py:80
  847.5 128.0 %reduce-scatter.22.cloned.1.call-start = ((), (), s32[]{:S(2)}) async-start(), calls=%async_computation.23 | async-start | bytes 5242880 | tf_op jit(solution)/shard_map/while/body/eval_jaxpr/reduce_scatter | solution.py:109
  897.4 80.8 %copy-start.27 = (f32[1,1,1,1024]{3,0,1,2:T(1,128)S(1)}, f32[1,1,1,1024]{3,0,1,2:T(1,128)}, u32[]{:S(2)}) copy-start(f32[1,1,1,1024]{3,0,1,2:T(1,128)} %get-tuple-element.819) | copy-start | bytes 12292 | tf_op jit(solution)/shard_map/while
  897.4 80.8 %copy-start.38 = (f32[1,1,1,1024]{3,0,1,2:T(1,128)S(1)}, f32[1,1,1,1024]{3,0,1,2:T(1,128)}, u32[]{:S(2)}) copy-start(f32[1,1,1,1024]{3,0,1,2:T(1,128)} %get-tuple-element.818) | copy-start | bytes 12292 | tf_op jit(solution)/shard_map/while
  897.4 108.3 %all-gather.31.cloned.1.call-start = ((), (), s32[]{:S(2)}) async-start(), calls=%async_computation.25 | async-start | bytes 2359296 | tf_op jit(solution)/shard_map/while/body/eval_jaxpr/all_gather | solution.py:52
  898.1 155.3 %all-gather.29.cloned.1.call-start = ((), (), s32[]{:S(2)}) async-start(), calls=%async_computation.24 | async-start | bytes 2621440 | tf_op jit(solution)/shard_map/while/body/eval_jaxpr/all_gather | solution.py:136
  900.2 181.8 %all-gather.35.cloned.1.call-start = ((), (), s32[]{:S(2)}) async-start(), calls=%async_computation.27 | async-start | bytes 2359296 | tf_op jit(solution)/shard_map/while/body/eval_jaxpr/all_gather | solution.py:51
  900.9 228.7 %all-gather.33.cloned.1.call-start = ((), (), s32[]{:S(2)}) async-start(), calls=%async_computation.26 | async-start | bytes 2621440 | tf_op jit(solution)/shard_map/while/body/eval_jaxpr/all_gather | solution.py:121
  979.2 206.8 %reduce-scatter.24.cloned.1.call-start = ((), (), s32[]{:S(2)}) async-start(), calls=%async_computation.28 | async-start | bytes 2621440 | tf_op jit(solution)/shard_map/while/body/eval_jaxpr/reduce_scatter | solution.py:151
  1143.4 87.7 %reduce-scatter.26.cloned.1.call-start = ((), (), s32[]{:S(2)}) async-start(), calls=%async_computation.29 | async-start | bytes 2621440 | tf_op jit(solution)/shard_map/while/body/eval_jaxpr/reduce_scatter | solution.py:129
  1150.4 130.9 %copy-start.11 = (bf16[1024,256]{1,0:T(8,128)(2,1)S(1)}, bf16[1024,256]{1,0:T(8,128)(2,1)}, u32[]{:S(2)}) copy-start(bf16[1024,256]{1,0:T(8,128)(2,1)} %all_gather.87) | copy-start | bytes 1572868 | tf_op jit(solution)/shard_map/while
  1150.4 130.9 %all-gather.37.cloned.1.call-start = ((), (), s32[]{:S(2)}) async-start(), calls=%async_computation.30 | async-start | bytes 2621440 | tf_op jit(solution)/shard_map/while/body/eval_jaxpr/all_gather | solution.py:161
  1236.2 134.9 %reduce-scatter.30.cloned.1.call-start = ((), (), s32[]{:S(2)}) async-start(), calls=%async_computation.32 | async-start | bytes 1572864 | tf_op jit(solution)/shard_map/while/body/eval_jaxpr/reduce_scatter | solution.py:213
  1363.8 19.2 %reduce-scatter.28.cloned.1.call-start = ((), (), s32[]{:S(2)}) async-start(), calls=%async_computation.31 | async-start | bytes 1572864 | tf_op jit(solution)/shard_map/while/body/eval_jaxpr/reduce_scatter | solution.py:219
  1367.1 65.4 %reduce-scatter.32.cloned.1.call-start = ((), (), s32[]{:S(2)}) async-start(), calls=%async_computation.33 | async-start | bytes 2621440 | tf_op jit(solution)/shard_map/while/body/eval_jaxpr/reduce_scatter | solution.py:235
  1438.3 8.9 all-to-all-start.1
  1458.2 36.5 %reduce-scatter.14.cloned.1.call-start = ((), (), s32[]{:S(2)}) async-start(), calls=%async_computation.14 | async-start | bytes 589824 | tf_op jit(solution)/shard_map/reduce_scatter | solution.py:283
  1460.3 75.8 %reduce-scatter.12.cloned.1.call-start = ((), (), s32[]{:S(2)}) async-start(), calls=%async_computation.13 | async-start | bytes 1769472 | tf_op jit(solution)/shard_map/reduce_scatter | solution.py:280
  1463.6 116.7 %reduce-scatter.16.cloned.1.call-start = ((), (), s32[]{:S(2)}) async-start(), calls=%async_computation.15 | async-start | bytes 2359296 | tf_op jit(solution)/shard_map/reduce_scatter | solution.py:286
  1467.6 157.1 %reduce-scatter.18.cloned.1.call-start = ((), (), s32[]{:S(2)}) async-start(), calls=%async_computation.16 | async-start | bytes 2359296 | tf_op jit(solution)/shard_map/reduce_scatter | solution.py:289
  1471.6 202.4 %reduce-scatter.20.cloned.1.call-start = ((), (), s32[]{:S(2)}) async-start(), calls=%async_computation.17 | async-start | bytes 3538944 | tf_op jit(solution)/shard_map/reduce_scatter | solution.py:292
  (103 other events, 1691.6 us)
Sparse Core Ops, SparseCore 0:
  11.1 34.8 all-gather.18
  47.9 25.5 all-gather.22
  75.7 45.6 all-gather.20
  126.4 7.8 all-gather.24
  136.3 10.3 all-gather.26
  176.9 77.9 reduce-scatter.21
  256.8 28.2 all-gather.30
  287.3 45.6 all-gather.28
  334.8 26.5 all-gather.34
  363.5 45.6 all-gather.32
  423.0 42.4 reduce-scatter.23
  467.7 42.8 reduce-scatter.25
  515.8 44.8 all-gather.36
  643.3 7.1 reduce-scatter.29
  652.6 9.5 reduce-scatter.27
  666.9 44.8 reduce-scatter.31
  736.2 30.4 all-gather.18
  768.4 25.5 all-gather.22
  796.1 45.6 all-gather.20
  846.9 7.8 all-gather.24
  856.9 10.2 all-gather.26
  897.5 77.9 reduce-scatter.21
  977.4 28.2 all-gather.30
  1007.7 45.6 all-gather.28
  1055.3 26.5 all-gather.34
  1083.9 45.6 all-gather.32
  1143.5 42.4 reduce-scatter.23
  1188.3 42.8 reduce-scatter.25
  1236.4 44.8 all-gather.36
  1363.9 7.1 reduce-scatter.29
  1373.4 9.5 reduce-scatter.27
  1387.6 44.8 reduce-scatter.31
Sparse Core Ops, SparseCore 1:
  1462.3 32.3 reduce-scatter.13
  1497.9 38.2 reduce-scatter.11
  1539.3 40.9 reduce-scatter.15
  1583.6 41.0 reduce-scatter.17
  1628.0 45.9 reduce-scatter.19
where the time goes:
time: 1690 us; the launch traced here: 1680 us
  waiting for transfers between devices  1170 us (69%)
  matrix products  263 us (16%)
  other arithmetic  136 us (8%)
  local copies, waits for them, and re-layouts  57.8 us (3%)
  blocking collectives  21.7 us (1%)
  starting transfers between devices  18.6 us (1%)
    reduce_scatter x2, waiting for transfers between devices, one_clip(): lax.psum_scatter(partial_one.reshape(-1, patches_here, model_width), 'ten...  149 us
    all_gather x2, waiting for transfers between devices, one_clip(): gathered_one = lax.all_gather(entering_one, 'tensor', axis=0, tiled=True)  95.7 us
    all_gather x2, waiting for transfers between devices, one_clip(): lax.all_gather(grad_branch_two, 'tensor', axis=0, tiled=True)  95.5 us
    all_gather x2, waiting for transfers between devices, one_clip(): lax.all_gather(entering_two, 'tensor', axis=0, tiled=True)  95.4 us
    all_gather x2, waiting for transfers between devices, one_clip(): lax.all_gather(grad_branch_one, 'tensor', axis=0, tiled=True)  89.3 us
    reduce_scatter x2, waiting for transfers between devices, one_clip(): lax.psum_scatter(partial_two.reshape(-1, patches_here, model_width).astyp...  85.1 us
    reduce_scatter x2, waiting for transfers between devices, one_clip(): lax.psum_scatter(partial_back_two.astype(jnp.bfloat16), 'tensor', scatter...  71.1 us
    all_gather x2, waiting for transfers between devices, fetch_weights(): lax.all_gather(shards[4], ('dp', 'frame'), axis=0, tiled=True)  61.1 us
  transfers between devices with their start and end apart: 41, of which 39 were waited for; matrix products, arithmetic and copies ran while one was open for 8% of the time, Pallas kernels for 0%

commit v1 on v0

--- a/solution.py
+++ b/solution.py
@@ -7,6 +7,28 @@
 HEAD_DIM = 64
 epsilon = 1e-06
 highest = lax.Precision.HIGHEST
+
+
+def in_order(blocks, dim):
+    dims = list(blocks.shape[1:])
+    dims[dim] *= blocks.shape[0]
+    return jnp.moveaxis(blocks, 0, dim).reshape(dims)
+
+
+def collect(x, axis, dim):
+    size = lax.axis_size(axis)
+    pairs = [(i, (i + 1) % size) for i in range(size)]
+    back = [(b, a) for a, b in pairs]
+    lower, upper = ([], [])
+    for turn in range(size - 1):
+        if turn % 2 == 0:
+            lower.append(lax.ppermute(lower[-1] if lower else x, axis, pairs))
+        else:
+            upper.append(lax.ppermute(upper[-1] if upper else x, axis, back))
+    blocks = jnp.stack([*lower[::-1], x, *upper])
+    shift = lax.axis_index(axis) - len(lower)
+    blocks = blocks[(jnp.arange(size) - shift) % size]
+    return in_order(blocks, dim)
 
 
 def normalize(values):
@@ -133,9 +155,7 @@
             tiled=True,
         ).astype(jnp.float32)
         grad_branch_two = (modulation[:, 5] * upstream).astype(jnp.bfloat16)
-        grad_two_all = lax.all_gather(grad_branch_two, "tensor", axis=0, tiled=True).reshape(
-            token_count, model_width
-        )
+        grad_two_all = collect(grad_branch_two, "tensor", 0).reshape(token_count, model_width)
         output = (middle + modulation[:, 5] * branch_two).astype(jnp.bfloat16)
         grad_gate_two = jnp.sum(upstream * branch_two, axis=1)
         grad_hidden = jnp.dot(grad_two_all, downward_weight, preferred_element_type=jnp.float32)

time: 1690 us -> 1590 us (0.941)
  waiting for transfers between devices: 1170 us -> 1030 us
  starting transfers between devices: 18.6 us -> 43.8 us
    all_gather x2 -> x0, waiting for transfers between devices: 95.5 us -> none  [one_clip(): lax.all_gather(grad_branch_two, 'tensor', axis=0, tiled=True)]
    ppermute x0 -> x6, waiting for transfers between devices: none -> 47 us  [the longest x4 44.7 us: collect(): lower.append(lax.ppermute(lower[-1] if lower else x, axis, pairs))]
    all_gather x2, waiting for transfers between devices: 43.9 us -> 0.01 us  [fetch_weights(): lax.all_gather(shards[2], ('dp', 'frame'), axis=0, tiled=True)]
    all_gather x2, waiting for transfers between devices: 95.4 us -> 56.1 us  [one_clip(): lax.all_gather(entering_two, 'tensor', axis=0, tiled=True)]
    ppermute x0 -> x6, starting transfers between devices: none -> 26.3 us  [the longest x4 20.6 us: collect(): lower.append(lax.ppermute(lower[-1] if lower else x, axis, pairs))]
  transfers between devices with their start and end apart: 41 -> 45, of which waited for: 39 -> 41; matrix products, arithmetic and copies ran while one was open for 8% -> 9% of each run, Pallas kernels for 0% -> 0%
where the time goes in v1:
time: 1590 us
  waiting for transfers between devices  1030 us (65%)
  matrix products  259 us (16%)
  other arithmetic  143 us (9%)
  local copies, waits for them, and re-layouts  65 us (4%)
  starting transfers between devices  43.8 us (3%)
  blocking collectives  21.7 us (1%)
  between operations  16 us (1%)
    reduce_scatter x2, waiting for transfers between devices, one_clip(): lax.psum_scatter(partial_one.reshape(-1, patches_here, model_width), 'ten...  155 us
    all_gather x2, waiting for transfers between devices, one_clip(): gathered_one = lax.all_gather(entering_one, 'tensor', axis=0, tiled=True)  95.5 us
    all_gather x2, waiting for transfers between devices, one_clip(): lax.all_gather(grad_branch_one, 'tensor', axis=0, tiled=True)  89.5 us
    reduce_scatter x2, waiting for transfers between devices, one_clip(): lax.psum_scatter(partial_two.reshape(-1, patches_here, model_width).astyp...  85.1 us
    reduce_scatter x2, waiting for transfers between devices, one_clip(): lax.psum_scatter(partial_back_two.astype(jnp.bfloat16), 'tensor', scatter...  73.5 us
    all_gather x2, waiting for transfers between devices, fetch_weights(): lax.all_gather(shards[4], ('dp', 'frame'), axis=0, tiled=True)  61.1 us
    all_gather x2, waiting for transfers between devices, one_clip(): lax.all_gather(entering_two, 'tensor', axis=0, tiled=True)  56.1 us
    reduce_scatter x2, waiting for transfers between devices, one_clip(): lax.psum_scatter(partial_back_one.reshape(-1, patches_here, model_width)....  48.2 us
  transfers between devices with their start and end apart: 45, of which 41 were waited for; matrix products, arithmetic and copies ran while one was open for 9% of the time, Pallas kernels for 0%

profile of v1, /device:TPU:0, one launch (start us, length us, event | category | flops | bytes accessed | tf_op | source)
XLA Modules:
  0.0 1587.4 jit_solution(6003333558341568659)
XLA Ops:
  8.1 1353.7 %while.83 = (s32[]{:T(128)}, f32[1024,3,256]{2,0,1:T(8,128)}, f32[1024,256]{1,0:T(8,128)}, f32[1024,1024]{1,0:T(8,128)}, f32[1024,1024]{1,0:T(8,128)}, /*index=5...) while((s32[]{:T(128)}, f32[1024,3,256]{2,0,1:T(8,128)}, ...), condition=%wide.region_28.29_spmd.clone, body=%wide.region_0.28_spmd.clone.sunk | while | flops 23350259712 | bytes 687677632 | solution.py:298
  13.2 32.8 %all-gather.18.cloned.1.call-done = bf16[1024,6,256]{2,0,1:T(8,128)(2,1)} async-done(((bf16[128,6,256]{2,0,1:T(8,128)(2,1)}), bf16[1024,6,256]{2,0,1:T(8,128)(2,1)}) %all-gather.18.cloned.1.call-update) | async-done | bytes 3145744 | tf_op jit(solution)/shard_map/while/body/eval_jaxpr/all_gather | solution.py:75
  61.7 11.8 all-gather.22.cloned.1.call-done
  73.5 47.8 %all-gather.20.cloned.1.call-done = bf16[4,256,1024]{2,1,0:T(8,128)(2,1)} async-done(((bf16[1,256,1024]{2,1,0:T(8,128)(2,1)}), bf16[4,256,1024]{2,1,0:T(8,128)(2,1)}) %all-gather.20.cloned.1.call-update) | async-done | bytes 2097168 | tf_op jit(solution)/shard_map/while/body/eval_jaxpr/all_gather | solution.py:94
  126.9 10.8 all_gather.79
  148.1 20.5 %while.84 = (s32[]{:T(128)}, bf16[2,512,4,64]{1,3,2,0:T(8,128)(2,1)S(1)}, f32[2,4,512]{2,1,0:T(4,128)S(1)}, bf16[2,512,4,64]{1,3,2,0:T(8,128)(2,1)S(1)}, bf16[20...) while((s32[]{:T(128)}, bf16[2,512,4,64]{1,3,2,0:T(8,128)(2,1)S(1)}, ...), condition=%wide.region_6.6_spmd, body=%wide.region_3.5_spmd.sunk | while | flops 1111619584 | bytes 53018720 | solution.py:126
  177.6 77.3 %reduce-scatter.22.cloned.1.call-done = f32[1,256,1024]{2,1,0:T(8,128)} async-done(((f32[4,256,1024]{2,1,0:T(8,128)}), f32[1,256,1024]{2,1,0:T(8,128)}) %reduce-scatter.22.cloned.1.call-update) | async-done | bytes 1048592 | tf_op jit(solution)/shard_map/while/body/eval_jaxpr/reduce_scatter | solution.py:131
  265.0 12.3 collective-permute-done.1
  277.3 8.8 collective-permute-start.2
  288.4 9.9 collective-permute-done.2
  304.9 28.0 %all-gather.28.cloned.1.call-done = bf16[4,256,1024]{2,1,0:T(8,128)(2,1)} async-done(((bf16[1,256,1024]{2,1,0:T(8,128)(2,1)}), bf16[4,256,1024]{2,1,0:T(8,128)(2,1)}) %all-gather.28.cloned.1.call-update) | async-done | bytes 2097168 | tf_op jit(solution)/shard_map/while/body/eval_jaxpr/all_gather | solution.py:143
  339.4 22.3 %all-gather.32.cloned.1.call-done = bf16[1024,1024]{1,0:T(8,128)(2,1)} async-done(((bf16[128,1024]{1,0:T(8,128)(2,1)}), bf16[1024,1024]{1,0:T(8,128)(2,1)}) %all-gather.32.cloned.1.call-update) | async-done | bytes 2097168 | tf_op jit(solution)/shard_map/while/body/eval_jaxpr/all_gather | solution.py:74
  361.8 8.0 fusion.226
  380.6 36.7 %reduce-scatter.24.cloned.1.call-done = bf16[1,256,1024]{2,1,0:T(8,128)(2,1)} async-done(((bf16[4,256,1024]{2,1,0:T(8,128)(2,1)}), bf16[1,256,1024]{2,1,0:T(8,128)(2,1)}) %reduce-scatter.24.cloned.1.call-update) | async-done | bytes 524304 | tf_op jit(solution)/shard_map/while/body/eval_jaxpr/reduce_scatter | solution.py:171
  419.9 42.6 %reduce-scatter.26.cloned.1.call-done = bf16[1,256,1024]{2,1,0:T(8,128)(2,1)} async-done(((bf16[4,256,1024]{2,1,0:T(8,128)(2,1)}), bf16[1,256,1024]{2,1,0:T(8,128)(2,1)}) %reduce-scatter.26.cloned.1.call-update) | async-done | bytes 524304 | tf_op jit(solution)/shard_map/while/body/eval_jaxpr/reduce_scatter | solution.py:151
  467.9 44.8 %all-gather.34.cloned.1.call-done = bf16[4,256,1024]{2,1,0:T(8,128)(2,1)} async-done(((bf16[1,256,1024]{2,1,0:T(8,128)(2,1)}), bf16[4,256,1024]{2,1,0:T(8,128)(2,1)}) %all-gather.34.cloned.1.call-update) | async-done | bytes 2097168 | tf_op jit(solution)/shard_map/while/body/eval_jaxpr/all_gather | solution.py:181
  520.1 72.0 %while.85 = (s32[]{:T(128)}, f32[2048,4,64]{0,2,1:T(8,128)}, f32[2048,4,64]{0,2,1:T(8,128)}, bf16[2,512,4,64]{1,3,2,0:T(8,128)(2,1)}, bf16[2,512,4,64]{1,3,2,0:T...) while((s32[]{:T(128)}, f32[2048,4,64]{0,2,1:T(8,128)}, ...), condition=%wide.region_15.15_spmd.clone, body=%wide.region_13.14_spmd.clone.sunk | while | flops 2737436672 | bytes 176742640 | solution.py:229
  527.0 8.0 multiply_reduce_fusion.11
  535.0 10.5 multiply_convert_fusion.12
  562.7 8.0 multiply_reduce_fusion.11
  570.7 10.5 multiply_convert_fusion.12
  602.6 11.7 reduce-scatter.28.cloned.1.call-done
  638.1 25.7 %reduce-scatter.32.cloned.1.call-done = bf16[1,256,1024]{2,1,0:T(8,128)(2,1)} async-done(((bf16[4,256,1024]{2,1,0:T(8,128)(2,1)}), bf16[1,256,1024]{2,1,0:T(8,128)(2,1)}) %reduce-scatter.32.cloned.1.call-update) | async-done | bytes 524304 | tf_op jit(solution)/shard_map/while/body/eval_jaxpr/reduce_scatter | solution.py:255
  690.4 28.3 %all-gather.18.cloned.1.call-done = bf16[1024,6,256]{2,0,1:T(8,128)(2,1)} async-done(((bf16[128,6,256]{2,0,1:T(8,128)(2,1)}), bf16[1024,6,256]{2,0,1:T(8,128)(2,1)}) %all-gather.18.cloned.1.call-update) | async-done | bytes 3145744 | tf_op jit(solution)/shard_map/while/body/eval_jaxpr/all_gather | solution.py:75
  734.4 11.7 all-gather.22.cloned.1.call-done
  746.1 47.7 %all-gather.20.cloned.1.call-done = bf16[4,256,1024]{2,1,0:T(8,128)(2,1)} async-done(((bf16[1,256,1024]{2,1,0:T(8,128)(2,1)}), bf16[4,256,1024]{2,1,0:T(8,128)(2,1)}) %all-gather.20.cloned.1.call-update) | async-done | bytes 2097168 | tf_op jit(solution)/shard_map/while/body/eval_jaxpr/all_gather | solution.py:94
  799.4 10.8 all_gather.79
  820.5 20.5 %while.84 = (s32[]{:T(128)}, bf16[2,512,4,64]{1,3,2,0:T(8,128)(2,1)S(1)}, f32[2,4,512]{2,1,0:T(4,128)S(1)}, bf16[2,512,4,64]{1,3,2,0:T(8,128)(2,1)S(1)}, bf16[20...) while((s32[]{:T(128)}, bf16[2,512,4,64]{1,3,2,0:T(8,128)(2,1)S(1)}, ...), condition=%wide.region_6.6_spmd, body=%wide.region_3.5_spmd.sunk | while | flops 1111619584 | bytes 53018720 | solution.py:126
  850.0 77.3 %reduce-scatter.22.cloned.1.call-done = f32[1,256,1024]{2,1,0:T(8,128)} async-done(((f32[4,256,1024]{2,1,0:T(8,128)}), f32[1,256,1024]{2,1,0:T(8,128)}) %reduce-scatter.22.cloned.1.call-update) | async-done | bytes 1048592 | tf_op jit(solution)/shard_map/while/body/eval_jaxpr/reduce_scatter | solution.py:131
  937.1 12.5 collective-permute-done.1
  949.6 8.8 collective-permute-start.2
  960.7 9.9 collective-permute-done.2
  977.2 28.2 %all-gather.28.cloned.1.call-done = bf16[4,256,1024]{2,1,0:T(8,128)(2,1)} async-done(((bf16[1,256,1024]{2,1,0:T(8,128)(2,1)}), bf16[4,256,1024]{2,1,0:T(8,128)(2,1)}) %all-gather.28.cloned.1.call-update) | async-done | bytes 2097168 | tf_op jit(solution)/shard_map/while/body/eval_jaxpr/all_gather | solution.py:143
  1011.9 22.0 %all-gather.32.cloned.1.call-done = bf16[1024,1024]{1,0:T(8,128)(2,1)} async-done(((bf16[128,1024]{1,0:T(8,128)(2,1)}), bf16[1024,1024]{1,0:T(8,128)(2,1)}) %all-gather.32.cloned.1.call-update) | async-done | bytes 2097168 | tf_op jit(solution)/shard_map/while/body/eval_jaxpr/all_gather | solution.py:74
  1033.9 8.0 fusion.226
  1052.8 36.7 %reduce-scatter.24.cloned.1.call-done = bf16[1,256,1024]{2,1,0:T(8,128)(2,1)} async-done(((bf16[4,256,1024]{2,1,0:T(8,128)(2,1)}), bf16[1,256,1024]{2,1,0:T(8,128)(2,1)}) %reduce-scatter.24.cloned.1.call-update) | async-done | bytes 524304 | tf_op jit(solution)/shard_map/while/body/eval_jaxpr/reduce_scatter | solution.py:171
  1092.1 42.5 %reduce-scatter.26.cloned.1.call-done = bf16[1,256,1024]{2,1,0:T(8,128)(2,1)} async-done(((bf16[4,256,1024]{2,1,0:T(8,128)(2,1)}), bf16[1,256,1024]{2,1,0:T(8,128)(2,1)}) %reduce-scatter.26.cloned.1.call-update) | async-done | bytes 524304 | tf_op jit(solution)/shard_map/while/body/eval_jaxpr/reduce_scatter | solution.py:151
  1139.9 44.8 %all-gather.34.cloned.1.call-done = bf16[4,256,1024]{2,1,0:T(8,128)(2,1)} async-done(((bf16[1,256,1024]{2,1,0:T(8,128)(2,1)}), bf16[4,256,1024]{2,1,0:T(8,128)(2,1)}) %all-gather.34.cloned.1.call-update) | async-done | bytes 2097168 | tf_op jit(solution)/shard_map/while/body/eval_jaxpr/all_gather | solution.py:181
  1192.2 72.0 %while.85 = (s32[]{:T(128)}, f32[2048,4,64]{0,2,1:T(8,128)}, f32[2048,4,64]{0,2,1:T(8,128)}, bf16[2,512,4,64]{1,3,2,0:T(8,128)(2,1)}, bf16[2,512,4,64]{1,3,2,0:T...) while((s32[]{:T(128)}, f32[2048,4,64]{0,2,1:T(8,128)}, ...), condition=%wide.region_15.15_spmd.clone, body=%wide.region_13.14_spmd.clone.sunk | while | flops 2737436672 | bytes 176742640 | solution.py:229
  1207.0 10.5 multiply_convert_fusion.12
  1242.7 10.5 multiply_convert_fusion.12
  1274.6 11.9 reduce-scatter.28.cloned.1.call-done
  1313.5 22.5 %reduce-scatter.32.cloned.1.call-done = bf16[1,256,1024]{2,1,0:T(8,128)(2,1)} async-done(((bf16[4,256,1024]{2,1,0:T(8,128)(2,1)}), bf16[1,256,1024]{2,1,0:T(8,128)(2,1)}) %reduce-scatter.32.cloned.1.call-update) | async-done | bytes 524304 | tf_op jit(solution)/shard_map/while/body/eval_jaxpr/reduce_scatter | solution.py:255
  1380.0 18.4 %reduce-scatter.14.cloned.1.call-done = bf16[128,256]{1,0:T(8,128)(2,1)} async-done(((bf16[1024,256]{1,0:T(8,128)(2,1)}), bf16[128,256]{1,0:T(8,128)(2,1)}) %reduce-scatter.14.cloned.1.call-update) | async-done | bytes 65552 | tf_op jit(solution)/shard_map/reduce_scatter | solution.py:303
  1399.9 39.9 %reduce-scatter.12.cloned.1.call-done = bf16[128,3,256]{2,0,1:T(8,128)(2,1)} async-done(((bf16[1024,3,256]{2,0,1:T(8,128)(2,1)}), bf16[128,3,256]{2,0,1:T(8,128)(2,1)}) %reduce-scatter.12.cloned.1.call-update) | async-done | bytes 196624 | tf_op jit(solution)/shard_map/reduce_scatter | solution.py:300
  1441.5 42.4 %reduce-scatter.16.cloned.1.call-done = bf16[128,1024]{1,0:T(8,128)(2,1)} async-done(((bf16[1024,1024]{1,0:T(8,128)(2,1)}), bf16[128,1024]{1,0:T(8,128)(2,1)}) %reduce-scatter.16.cloned.1.call-update) | async-done | bytes 262160 | tf_op jit(solution)/shard_map/reduce_scatter | solution.py:306
  1485.7 42.5 %reduce-scatter.18.cloned.1.call-done = bf16[128,1024]{1,0:T(8,128)(2,1)} async-done(((bf16[1024,1024]{1,0:T(8,128)(2,1)}), bf16[128,1024]{1,0:T(8,128)(2,1)}) %reduce-scatter.18.cloned.1.call-update) | async-done | bytes 262160 | tf_op jit(solution)/shard_map/reduce_scatter | solution.py:309
  1530.0 47.6 %reduce-scatter.20.cloned.1.call-done = bf16[128,6,256]{2,0,1:T(8,128)(2,1)} async-done(((bf16[1024,6,256]{2,0,1:T(8,128)(2,1)}), bf16[128,6,256]{2,0,1:T(8,128)(2,1)}) %reduce-scatter.20.cloned.1.call-update) | async-done | bytes 393232 | tf_op jit(solution)/shard_map/reduce_scatter | solution.py:312
  (519 shorter events, 462.5 us)
Async XLA Ops:
  8.3 37.7 %all-gather.18.cloned.1.call-start = ((), (), s32[]{:S(2)}) async-start(), calls=%async_computation.18 | async-start | bytes 3538944 | tf_op jit(solution)/shard_map/while/body/eval_jaxpr/all_gather | solution.py:75
  9.1 64.4 %all-gather.22.cloned.1.call-start = ((), (), s32[]{:S(2)}) async-start(), calls=%async_computation.20 | async-start | bytes 1769472 | tf_op jit(solution)/shard_map/while/body/eval_jaxpr/all_gather | solution.py:71
  11.7 113.4 %copy-start.33 = (f32[256]{0:T(256)}, f32[256]{0:T(256)S(1)}, u32[]{:S(2)}) copy-start(f32[256]{0:T(256)S(1)} %broadcast_multiply_fusion.11) | copy-start | bytes 3076 | tf_op jit(solution)/shard_map/while
  49.0 10.3 all-to-all-start
  53.6 67.7 %all-gather.20.cloned.1.call-start = ((), (), s32[]{:S(2)}) async-start(), calls=%async_computation.19 | async-start | bytes 2621440 | tf_op jit(solution)/shard_map/while/body/eval_jaxpr/all_gather | solution.py:94
  61.6 77.2 %all-gather.24.cloned.1.call-start = ((), (), s32[]{:S(2)}) async-start(), calls=%async_computation.21 | async-start | bytes 1572864 | tf_op jit(solution)/shard_map/while/body/eval_jaxpr/all_gather | solution.py:101
  126.3 20.3 %all-gather.26.cloned.1.call-start = ((), (), s32[]{:S(2)}) async-start(), calls=%async_computation.22 | async-start | bytes 1572864 | tf_op jit(solution)/shard_map/while/body/eval_jaxpr/all_gather | solution.py:102
  126.9 128.0 %reduce-scatter.22.cloned.1.call-start = ((), (), s32[]{:S(2)}) async-start(), calls=%async_computation.23 | async-start | bytes 5242880 | tf_op jit(solution)/shard_map/while/body/eval_jaxpr/reduce_scatter | solution.py:131
  176.7 128.2 %all-gather.30.cloned.1.call-start = ((), (), s32[]{:S(2)}) async-start(), calls=%async_computation.25 | async-start | bytes 2359296 | tf_op jit(solution)/shard_map/while/body/eval_jaxpr/all_gather | solution.py:73
  177.5 155.4 %all-gather.28.cloned.1.call-start = ((), (), s32[]{:S(2)}) async-start(), calls=%async_computation.24 | async-start | bytes 2621440 | tf_op jit(solution)/shard_map/while/body/eval_jaxpr/all_gather | solution.py:143
  258.5 103.2 %all-gather.32.cloned.1.call-start = ((), (), s32[]{:S(2)}) async-start(), calls=%async_computation.26 | async-start | bytes 2359296 | tf_op jit(solution)/shard_map/while/body/eval_jaxpr/all_gather | solution.py:74
  259.3 158.1 %reduce-scatter.24.cloned.1.call-start = ((), (), s32[]{:S(2)}) async-start(), calls=%async_computation.27 | async-start | bytes 2621440 | tf_op jit(solution)/shard_map/while/body/eval_jaxpr/reduce_scatter | solution.py:171
  260.5 16.8 %collective-permute-start.1 = (bf16[1,256,1024]{2,1,0:T(8,128)(2,1)S(1)}, bf16[1,256,1024]{2,1,0:T(8,128)(2,1)}, u32[]{:S(2)}, u32[]{:S(2)}) collective-permute-start(bf16[1,256,1024]{2,1,0:T(8,128)(2,1)S(1)} %fusion.223), channel_id=1, source_target_pairs={{0,1},{1,2},{2,3},{3,0},{4,5},{5,6},{6,7},{7,4},{8,9},{9,10},{10,1... | collective-permute-start | bytes 1572872 | tf_op jit(solution)/shard_map/while/body/eval_jaxpr/ppermute | solution.py:25
  262.0 26.4 %collective-permute-start = (bf16[1,256,1024]{2,1,0:T(8,128)(2,1)S(1)}, bf16[1,256,1024]{2,1,0:T(8,128)(2,1)}, u32[]{:S(2)}, u32[]{:S(2)}) collective-permute-start(bf16[1,256,1024]{2,1,0:T(8,128)(2,1)S(1)} %fusion.223), channel_id=1, source_target_pairs={{1,0},{2,1},{3,2},{0,3},{5,4},{6,5},{7,6},{4,7},{9,8},{10,9},{11,1... | collective-permute-start | bytes 1572872 | tf_op jit(solution)/shard_map/while/body/eval_jaxpr/ppermute | solution.py:27
  277.3 21.1 %collective-permute-start.2 = (bf16[1,256,1024]{2,1,0:T(8,128)(2,1)}, bf16[1,256,1024]{2,1,0:T(8,128)(2,1)}, u32[]{:S(2)}, u32[]{:S(2)}) collective-permute-start(bf16[1,256,1024]{2,1,0:T(8,128)(2,1)} %collective-permute-done.1), channel_id=1, source_target_pairs={{0,1},{1,2},{2,3},{3,0},{4,5},{5,6},{6,7},{7,4},{8,9},{9,10},{10,1... | collective-permute-start | bytes 1572872 | tf_op jit(solution)/shard_map/while/body/eval_jaxpr/ppermute | solution.py:25
  373.6 88.9 %reduce-scatter.26.cloned.1.call-start = ((), (), s32[]{:S(2)}) async-start(), calls=%async_computation.28 | async-start | bytes 2621440 | tf_op jit(solution)/shard_map/while/body/eval_jaxpr/reduce_scatter | solution.py:151
  380.6 132.1 %copy-start.11 = (bf16[1024,256]{1,0:T(8,128)(2,1)S(1)}, bf16[1024,256]{1,0:T(8,128)(2,1)}, u32[]{:S(2)}) copy-start(bf16[1024,256]{1,0:T(8,128)(2,1)} %all_gather.79) | copy-start | bytes 1572868 | tf_op jit(solution)/shard_map/while
  380.6 132.1 %all-gather.34.cloned.1.call-start = ((), (), s32[]{:S(2)}) async-start(), calls=%async_computation.29 | async-start | bytes 2621440 | tf_op jit(solution)/shard_map/while/body/eval_jaxpr/all_gather | solution.py:181
  467.7 134.9 %reduce-scatter.30.cloned.1.call-start = ((), (), s32[]{:S(2)}) async-start(), calls=%async_computation.31 | async-start | bytes 1572864 | tf_op jit(solution)/shard_map/while/body/eval_jaxpr/reduce_scatter | solution.py:233
  595.3 19.1 %reduce-scatter.28.cloned.1.call-start = ((), (), s32[]{:S(2)}) async-start(), calls=%async_computation.30 | async-start | bytes 1572864 | tf_op jit(solution)/shard_map/while/body/eval_jaxpr/reduce_scatter | solution.py:239
  598.5 65.3 %reduce-scatter.32.cloned.1.call-start = ((), (), s32[]{:S(2)}) async-start(), calls=%async_computation.32 | async-start | bytes 2621440 | tf_op jit(solution)/shard_map/while/body/eval_jaxpr/reduce_scatter | solution.py:255
  669.8 8.9 all-to-all-start.1
  685.8 32.9 %all-gather.18.cloned.1.call-start = ((), (), s32[]{:S(2)}) async-start(), calls=%async_computation.18 | async-start | bytes 3538944 | tf_op jit(solution)/shard_map/while/body/eval_jaxpr/all_gather | solution.py:75
  686.4 59.7 %all-gather.22.cloned.1.call-start = ((), (), s32[]{:S(2)}) async-start(), calls=%async_computation.20 | async-start | bytes 1769472 | tf_op jit(solution)/shard_map/while/body/eval_jaxpr/all_gather | solution.py:71
  721.8 10.3 all-to-all-start
  726.4 67.4 %all-gather.20.cloned.1.call-start = ((), (), s32[]{:S(2)}) async-start(), calls=%async_computation.19 | async-start | bytes 2621440 | tf_op jit(solution)/shard_map/while/body/eval_jaxpr/all_gather | solution.py:94
  734.4 76.9 %all-gather.24.cloned.1.call-start = ((), (), s32[]{:S(2)}) async-start(), calls=%async_computation.21 | async-start | bytes 1572864 | tf_op jit(solution)/shard_map/while/body/eval_jaxpr/all_gather | solution.py:101
  798.7 20.3 %all-gather.26.cloned.1.call-start = ((), (), s32[]{:S(2)}) async-start(), calls=%async_computation.22 | async-start | bytes 1572864 | tf_op jit(solution)/shard_map/while/body/eval_jaxpr/all_gather | solution.py:102
  799.3 128.0 %reduce-scatter.22.cloned.1.call-start = ((), (), s32[]{:S(2)}) async-start(), calls=%async_computation.23 | async-start | bytes 5242880 | tf_op jit(solution)/shard_map/while/body/eval_jaxpr/reduce_scatter | solution.py:131
  849.2 128.0 %all-gather.30.cloned.1.call-start = ((), (), s32[]{:S(2)}) async-start(), calls=%async_computation.25 | async-start | bytes 2359296 | tf_op jit(solution)/shard_map/while/body/eval_jaxpr/all_gather | solution.py:73
  850.0 155.4 %all-gather.28.cloned.1.call-start = ((), (), s32[]{:S(2)}) async-start(), calls=%async_computation.24 | async-start | bytes 2621440 | tf_op jit(solution)/shard_map/while/body/eval_jaxpr/all_gather | solution.py:143
  931.0 102.9 %all-gather.32.cloned.1.call-start = ((), (), s32[]{:S(2)}) async-start(), calls=%async_computation.26 | async-start | bytes 2359296 | tf_op jit(solution)/shard_map/while/body/eval_jaxpr/all_gather | solution.py:74
  931.6 158.0 %reduce-scatter.24.cloned.1.call-start = ((), (), s32[]{:S(2)}) async-start(), calls=%async_computation.27 | async-start | bytes 2621440 | tf_op jit(solution)/shard_map/while/body/eval_jaxpr/reduce_scatter | solution.py:171
  932.8 16.8 %collective-permute-start.1 = (bf16[1,256,1024]{2,1,0:T(8,128)(2,1)S(1)}, bf16[1,256,1024]{2,1,0:T(8,128)(2,1)}, u32[]{:S(2)}, u32[]{:S(2)}) collective-permute-start(bf16[1,256,1024]{2,1,0:T(8,128)(2,1)S(1)} %fusion.223), channel_id=1, source_target_pairs={{0,1},{1,2},{2,3},{3,0},{4,5},{5,6},{6,7},{7,4},{8,9},{9,10},{10,1... | collective-permute-start | bytes 1572872 | tf_op jit(solution)/shard_map/while/body/eval_jaxpr/ppermute | solution.py:25
  934.3 26.4 %collective-permute-start = (bf16[1,256,1024]{2,1,0:T(8,128)(2,1)S(1)}, bf16[1,256,1024]{2,1,0:T(8,128)(2,1)}, u32[]{:S(2)}, u32[]{:S(2)}) collective-permute-start(bf16[1,256,1024]{2,1,0:T(8,128)(2,1)S(1)} %fusion.223), channel_id=1, source_target_pairs={{1,0},{2,1},{3,2},{0,3},{5,4},{6,5},{7,6},{4,7},{9,8},{10,9},{11,1... | collective-permute-start | bytes 1572872 | tf_op jit(solution)/shard_map/while/body/eval_jaxpr/ppermute | solution.py:27
  949.6 21.1 %collective-permute-start.2 = (bf16[1,256,1024]{2,1,0:T(8,128)(2,1)}, bf16[1,256,1024]{2,1,0:T(8,128)(2,1)}, u32[]{:S(2)}, u32[]{:S(2)}) collective-permute-start(bf16[1,256,1024]{2,1,0:T(8,128)(2,1)} %collective-permute-done.1), channel_id=1, source_target_pairs={{0,1},{1,2},{2,3},{3,0},{4,5},{5,6},{6,7},{7,4},{8,9},{9,10},{10,1... | collective-permute-start | bytes 1572872 | tf_op jit(solution)/shard_map/while/body/eval_jaxpr/ppermute | solution.py:25
  1045.8 88.8 %reduce-scatter.26.cloned.1.call-start = ((), (), s32[]{:S(2)}) async-start(), calls=%async_computation.28 | async-start | bytes 2621440 | tf_op jit(solution)/shard_map/while/body/eval_jaxpr/reduce_scatter | solution.py:151
  1052.8 131.9 %copy-start.11 = (bf16[1024,256]{1,0:T(8,128)(2,1)S(1)}, bf16[1024,256]{1,0:T(8,128)(2,1)}, u32[]{:S(2)}) copy-start(bf16[1024,256]{1,0:T(8,128)(2,1)} %all_gather.79) | copy-start | bytes 1572868 | tf_op jit(solution)/shard_map/while
  1052.8 131.9 %all-gather.34.cloned.1.call-start = ((), (), s32[]{:S(2)}) async-start(), calls=%async_computation.29 | async-start | bytes 2621440 | tf_op jit(solution)/shard_map/while/body/eval_jaxpr/all_gather | solution.py:181
  1139.7 134.9 %reduce-scatter.30.cloned.1.call-start = ((), (), s32[]{:S(2)}) async-start(), calls=%async_computation.31 | async-start | bytes 1572864 | tf_op jit(solution)/shard_map/while/body/eval_jaxpr/reduce_scatter | solution.py:233
  1267.3 19.2 %reduce-scatter.28.cloned.1.call-start = ((), (), s32[]{:S(2)}) async-start(), calls=%async_computation.30 | async-start | bytes 1572864 | tf_op jit(solution)/shard_map/while/body/eval_jaxpr/reduce_scatter | solution.py:239
  1270.6 65.5 %reduce-scatter.32.cloned.1.call-start = ((), (), s32[]{:S(2)}) async-start(), calls=%async_computation.32 | async-start | bytes 2621440 | tf_op jit(solution)/shard_map/while/body/eval_jaxpr/reduce_scatter | solution.py:255
  1342.0 8.9 all-to-all-start.1
  1361.8 36.6 %reduce-scatter.14.cloned.1.call-start = ((), (), s32[]{:S(2)}) async-start(), calls=%async_computation.14 | async-start | bytes 589824 | tf_op jit(solution)/shard_map/reduce_scatter | solution.py:303
  1364.0 75.8 %reduce-scatter.12.cloned.1.call-start = ((), (), s32[]{:S(2)}) async-start(), calls=%async_computation.13 | async-start | bytes 1769472 | tf_op jit(solution)/shard_map/reduce_scatter | solution.py:300
  1367.2 116.7 %reduce-scatter.16.cloned.1.call-start = ((), (), s32[]{:S(2)}) async-start(), calls=%async_computation.15 | async-start | bytes 2359296 | tf_op jit(solution)/shard_map/reduce_scatter | solution.py:306
  1371.1 157.1 %reduce-scatter.18.cloned.1.call-start = ((), (), s32[]{:S(2)}) async-start(), calls=%async_computation.16 | async-start | bytes 2359296 | tf_op jit(solution)/shard_map/reduce_scatter | solution.py:309
  1375.1 202.5 %reduce-scatter.20.cloned.1.call-start = ((), (), s32[]{:S(2)}) async-start(), calls=%async_computation.17 | async-start | bytes 3538944 | tf_op jit(solution)/shard_map/reduce_scatter | solution.py:312
  (107 other events, 2203.2 us)
Sparse Core Ops, SparseCore 0:
  11.0 34.8 all-gather.17
  47.9 25.5 all-gather.21
  75.6 45.6 all-gather.19
  126.4 7.8 all-gather.23
  136.2 10.3 all-gather.25
  176.9 77.9 reduce-scatter.21
  256.8 28.2 all-gather.29
  287.2 45.6 all-gather.27
  334.8 26.9 all-gather.31
  373.7 43.6 reduce-scatter.23
  419.7 42.8 reduce-scatter.25
  467.8 44.8 all-gather.33
  595.4 7.1 reduce-scatter.29
  604.7 9.5 reduce-scatter.27
  618.9 44.8 reduce-scatter.31
  688.2 30.4 all-gather.17
  720.5 25.5 all-gather.21
  748.1 45.6 all-gather.19
  798.8 7.8 all-gather.23
  808.7 10.3 all-gather.25
  849.3 77.9 reduce-scatter.21
  929.2 28.2 all-gather.29
  959.7 45.6 all-gather.27
  1007.1 26.7 all-gather.31
  1045.9 43.6 reduce-scatter.23
  1091.7 42.8 reduce-scatter.25
  1139.8 44.8 all-gather.33
  1267.4 7.1 reduce-scatter.29
  1276.9 9.5 reduce-scatter.27
  1291.1 44.8 reduce-scatter.31
Sparse Core Ops, SparseCore 1:
  1365.9 32.4 reduce-scatter.13
  1401.5 38.2 reduce-scatter.11
  1442.9 40.9 reduce-scatter.15
  1487.2 41.0 reduce-scatter.17
  1531.7 45.9 reduce-scatter.19
